TPU v7x, 768 devices: a whole 4x8x12 slice. The times are simulated.
768 devices in a mesh: section: 16 (over y, core), tensor: 4 (over z_lo), dp: 12 (over z_hi, x).
Axes of the slice: x: 4, y: 8, z: 12 (z_hi: 3, z_lo: 4; z = z_hi * 4 + z_lo), core: 2. Of those that a mesh axis runs over, the one named last changes fastest.
Arguments:
- acts: bfloat16 [16, 24, 256, 2048], P('section', 'dp', 'tensor'), parts along dimension 1, may hold values from -6 to 6
- fresh: bfloat16 [24, 256, 2048], P('dp', 'tensor'), parts along dimension 0, may hold values from -6 to 6
- order: int32 [16, 2], P('section'), may hold values from 0 to 1
- ln_gain: float32 [16, 2048], P('section'), may hold values from 0.1 to 1.9
- ln_bias: float32 [16, 2048], P('section'), may hold values from -3 to 3
- wqkv: bfloat16 [16, 2048, 6144], P('section', None, 'tensor'), may hold values from -4 to 4
- wo: bfloat16 [16, 2048, 2048], P('section', 'tensor'), may hold values from -0.125 to 0.125
Outputs:
- section_out: bfloat16 [24, 16, 256, 2048], P('dp', 'section', 'tensor'), parts along dimension 0
- held: bfloat16 [16, 24, 256, 2048], P('section', 'dp', 'tensor'), parts along dimension 1
There are 12 independent parts, one for each index of `dp`. A program takes and returns all parts, laid end to end along the dimension named above; an argument that names none is the same for every part. Nothing has to cross between parts.
All inputs are finite; a program needn't handle non-finite values.
Results may differ from a plain program's by a relative error of at most 0.017.
Values may be sent and summed in bfloat16 or wider, within the bound.
A program may use at most 64 MiB of HBM per device.

v0:
```python
import jax
import jax.numpy as jnp
from jax import lax
from jax.sharding import PartitionSpec as P

HD = 128
TICKS = 2


def in_order(pieces, dim):
    shape = list(pieces.shape[1:])
    shape[dim] *= pieces.shape[0]
    return jnp.moveaxis(pieces, 0, dim).reshape(shape)


def from_everyone(array, axis):
    length = lax.axis_size(axis)
    return lax.all_to_all(
        jnp.broadcast_to(array[None], (length, *array.shape)), axis, 0, 0, tiled=True
    )


def gathered_copies(array, axis, dim):
    return in_order(from_everyone(array, axis), dim)


def split_up(array, dim, length):
    before, after = (array.shape[:dim], array.shape[dim + 1 :])
    return jnp.moveaxis(array.reshape(*before, length, -1, *after), dim, 0)


def summed_on_arrival(array, axis, dim):
    length = lax.axis_size(axis)
    pieces = lax.all_to_all(split_up(array, dim, length), axis, 0, 0, tiled=True)
    return jnp.sum(pieces.astype(jnp.float32), axis=0)


def from_behind(block, axis, distance):
    devices = range(lax.axis_size(axis))
    route = [(i - distance, i) for i in devices if i - distance in devices]
    return lax.ppermute(block, axis, route)


def normed(rows, gain, bias):
    values = rows.astype(jnp.float32)
    centred = values - jnp.mean(values, axis=-1, keepdims=True)
    spread = jnp.mean(centred * centred, axis=-1, keepdims=True)
    return (centred * lax.rsqrt(spread + 1e-06) * gain + bias).astype(jnp.bfloat16)


def attend(qkv):
    length = qkv.shape[0]
    local_heads = qkv.shape[1] // (3 * HD)
    grid = qkv.reshape(length, local_heads, 3, HD)
    scores = jnp.einsum(
        "qhe,khe->hqk", grid[:, :, 0], grid[:, :, 1], preferred_element_type=jnp.float32
    )
    scores = scores / jnp.sqrt(jnp.float32(HD))
    probs = jax.nn.softmax(scores, axis=-1).astype(jnp.bfloat16)
    mixed = jnp.einsum("hqk,khe->qhe", probs, grid[:, :, 2], preferred_element_type=jnp.float32)
    return mixed.astype(jnp.bfloat16).reshape(length, local_heads * HD)


def body(acts, fresh, order, ln_gain, ln_bias, wqkv, wo):
    gain = ln_gain[0]
    bias = ln_bias[0]
    w_in = wqkv[0]
    w_out = wo[0]
    first = lax.axis_index("section") == 0
    slot_ids = jnp.arange(acts.shape[1], dtype=jnp.int32)
    outputs = []
    slots = acts[0]
    for tick in range(TICKS):
        chosen = order[0, tick]
        current = lax.dynamic_index_in_dim(slots, chosen, 0, keepdims=False)
        qkv = jnp.dot(
            normed(gathered_copies(current, "tensor", 0), gain, bias),
            w_in,
            preferred_element_type=jnp.float32,
        ).astype(jnp.bfloat16)
        mixed = attend(qkv)
        total = summed_on_arrival(
            jnp.dot(mixed, w_out, preferred_element_type=jnp.float32).astype(jnp.bfloat16),
            "tensor",
            0,
        )
        result = (current.astype(jnp.float32) + total).astype(jnp.bfloat16)
        outputs.append(result)
        arriving = from_behind(result, "section", 1)
        arriving = jnp.where(first, fresh[tick], arriving)
        slots = jnp.where((slot_ids == chosen)[:, None, None], arriving[None], slots)
    return (jnp.stack(outputs, axis=0)[:, None], slots[None])


def solution(mesh):
    return jax.shard_map(
        body,
        mesh=mesh,
        in_specs=(
            P("section", "dp", "tensor", None),
            P("dp", "tensor", None),
            P("section", None),
            P("section", None),
            P("section", None),
            P("section", None, "tensor"),
            P("section", "tensor", None),
        ),
        out_specs=(P("dp", "section", "tensor", None), P("section", "dp", "tensor", None)),
        check_vma=False,
    )
```

profile of v0, /device:TPU:1, one launch (start us, length us, event | category | flops | bytes accessed | tf_op | source)
XLA Modules:
  0.0 172.3 jit_solution(16619220975304339969)
XLA Ops:
  0.6 0.0 copy-start
  0.6 1.4 fusion.37
  4.0 1.0 dynamic-slice_bitcast_fusion
  5.0 0.1 broadcast_in_dim.63
  5.1 0.0 copy-start.5
  5.1 0.0 copy-start.6
  5.1 0.0 copy-start.7
  5.1 31.2 %all_to_all.20 = bf16[4,64,2048]{2,1,0:T(8,128)(2,1)S(1)} all-to-all(bf16[4,64,2048]{2,1,0:T(8,128)(2,1)S(1)} %broadcast_in_dim.63), channel_id=1, replica_groups=mesh['section'=16,'tensor'=4,'dp'=12] {'tensor'}, dimensions={0} | all-to-all | bytes 2097152 | tf_op jit(solution)/shard_map/all_to_all | solution.py:18
  36.3 0.2 convert_reduce_fusion.1
  36.6 0.4 fusion.20
  37.0 0.0 copy-done.5
  37.0 0.0 copy-done.6
  37.0 0.5 fusion.23
  37.5 0.0 copy-done.7
  37.5 2.7 %fusion.6 = bf16[256,1536]{1,0:T(8,128)(2,1)} fusion(bf16[256,2048]{1,0:T(8,128)(2,1)S(1)} %bitcast.110, bf16[1,2048,1536]{2,1,0:T(8,128)(2,1)S(1)} %copy-done.7), kind=kOutput, calls=%fused_computation.12 | convolution fusion | flops 1611005952 | bytes 8126464 | tf_op jit(solution)/shard_map/dot_general | solution.py:76
  40.2 1.4 copy.27
  41.6 0.5 fusion.38
  42.1 1.3 convolution_multiply_fusion.1
  43.4 2.0 %convolution_convert_fusion.3 = bf16[4,128,256]{2,1,0:T(8,128)(2,1)S(1)} fusion(f32[4,256]{1,0:T(4,128)S(1)} %fusion.38, bf16[256,4,3,128]{0,3,2,1:T(8,128)(2,1)S(1)} %bitcast.106, f32[4,256,256]{1,2,0:T(8,128)} %convolution_multiply_fusion.1), kind=kOutput, calls=%fused_computation.37 | convolution fusion | flops 68027648 | bytes 2625536 | tf_op jit(solution)/shard_map/hqk,khe->qhe/dot_general | solution.py:60
  45.4 0.0 copy-done
  45.4 0.7 convolution_convert_fusion.1
  46.1 0.0 copy-start.1
  46.2 27.9 %all_to_all.21 = bf16[4,64,2048]{2,1,0:T(8,128)(2,1)S(1)} all-to-all(bf16[4,64,2048]{2,1,0:T(8,128)(2,1)S(1)} %bitcast.103), channel_id=1, replica_groups=mesh['section'=16,'tensor'=4,'dp'=12] {'tensor'}, dimensions={0} | all-to-all | bytes 2097152 | tf_op jit(solution)/shard_map/all_to_all | solution.py:34
  74.1 0.2 convert_reduce_fusion.3
  74.2 0.0 copy-done.1
  74.2 0.1 add_convert_fusion.1
  74.3 6.5 %collective-permute-start = (bf16[64,2048]{1,0:T(8,128)(2,1)S(1)}, bf16[64,2048]{1,0:T(8,128)(2,1)}, u32[]{:S(2)}, u32[]{:S(2)}) collective-permute-start(bf16[64,2048]{1,0:T(8,128)(2,1)S(1)} %add_convert_fusion.1), channel_id=1, source_target_pairs={{0,48},{48,96},{96,144},{144,192},{192,240},{240,288},{288,336},{3... | collective-permute-start | bytes 786440 | tf_op jit(solution)/shard_map/ppermute | solution.py:41
  82.6 0.7 iota_compare_fusion.1
  83.3 0.6 dynamic-slice.1
  83.9 0.2 collective-permute-done
  84.1 1.1 bitcast_select_fusion.1
  85.2 0.6 fusion.32
  85.8 0.0 copy-start.2
  85.8 0.1 broadcast_in_dim.67
  85.9 26.2 %all_to_all.22 = bf16[4,64,2048]{2,1,0:T(8,128)(2,1)S(1)} all-to-all(bf16[4,64,2048]{2,1,0:T(8,128)(2,1)S(1)} %broadcast_in_dim.67), channel_id=1, replica_groups=mesh['section'=16,'tensor'=4,'dp'=12] {'tensor'}, dimensions={0} | all-to-all | bytes 2097152 | tf_op jit(solution)/shard_map/all_to_all | solution.py:18
  112.2 0.2 convert_reduce_fusion
  112.4 0.0 copy-done.2
  112.4 0.4 fusion.16
  112.8 0.5 fusion.19
  113.3 5.5 %fusion.9 = bf16[256,1536]{1,0:T(8,128)(2,1)} fusion(bf16[256,2048]{1,0:T(8,128)(2,1)S(1)} %bitcast.111, bf16[1,2048,1536]{2,1,0:T(8,128)(2,1)} %param.12), kind=kOutput, calls=%fused_computation.13 | convolution fusion | flops 1611005952 | bytes 8126464 | tf_op jit(solution)/shard_map/dot_general | solution.py:76
  118.8 2.3 %copy.32 = bf16[256,1536]{0,1:T(8,128)(2,1)} copy(bf16[256,1536]{1,0:T(8,128)(2,1)} %fusion.9) | data formatting | bytes 1572864 | tf_op jit(solution)/shard_map/convert_element_type | solution.py:80
  121.1 1.5 fusion.39
  122.6 2.4 %convolution_multiply_fusion = f32[4,256,256]{1,2,0:T(8,128)} fusion(bf16[256,4,3,128]{0,3,2,1:T(8,128)(2,1)} %bitcast.108), kind=kOutput, calls=%fused_computation.34 | convolution fusion | flops 67371008 | bytes 1572864 | tf_op jit(solution)/shard_map/qhe,khe->hqk/dot_general | solution.py:55
  125.0 2.8 %convolution_convert_fusion.2 = bf16[4,128,256]{2,1,0:T(8,128)(2,1)} fusion(f32[4,256]{1,0:T(4,128)S(1)} %fusion.39, bf16[256,4,3,128]{0,3,2,1:T(8,128)(2,1)} %bitcast.109, f32[4,256,256]{1,2,0:T(8,128)} %convolution_multiply_fusion), kind=kOutput, calls=%fused_computation.36 | convolution fusion | flops 68027648 | bytes 2625536 | tf_op jit(solution)/shard_map/hqk,khe->qhe/dot_general | solution.py:60
  127.8 2.7 %convolution_convert_fusion = bf16[256,2048]{1,0:T(8,128)(2,1)} fusion(bf16[256,512]{0,1:T(8,128)(2,1)} %bitcast.113, bf16[1,512,2048]{2,1,0:T(8,128)(2,1)S(1)} %copy-done), kind=kOutput, calls=%fused_computation.10 | convolution fusion | flops 537395200 | bytes 3407872 | tf_op jit(solution)/shard_map/dot_general | solution.py:83
  130.5 4.2 %all-to-all-start.3 = ((bf16[4,64,2048]{2,1,0:T(8,128)(2,1)}), bf16[4,64,2048]{2,1,0:T(8,128)(2,1)}, u32[]{:S(2)}, u32[]{:S(2)}) async-start(bf16[4,64,2048]{2,1,0:T(8,128)(2,1)} %bitcast.102), calls=%async_computation.3 | async-start | bytes 2097152 | tf_op jit(solution)/shard_map/all_to_all | solution.py:34
  134.8 0.6 iota_compare_fusion
  135.4 0.8 fusion.30
  136.1 0.0 copy-start.3
  136.1 24.8 %all-to-all-done.3 = bf16[4,64,2048]{2,1,0:T(8,128)(2,1)} async-done(((bf16[4,64,2048]{2,1,0:T(8,128)(2,1)}), bf16[4,64,2048]{2,1,0:T(8,128)(2,1)}, u32[]{:S(2)}, u32[]{:S(2)}) %all-to-all-start.3) | async-done | bytes 1048608 | tf_op jit(solution)/shard_map/all_to_all | solution.py:34
  160.9 1.4 convert_reduce_fusion.2
  162.3 0.0 copy-start.4
  162.4 1.1 add_convert_fusion
  163.4 4.6 %collective-permute-start.1 = (bf16[64,2048]{1,0:T(8,128)(2,1)S(1)}, bf16[64,2048]{1,0:T(8,128)(2,1)S(1)}, u32[]{:S(2)}, u32[]{:S(2)}) collective-permute-start(bf16[64,2048]{1,0:T(8,128)(2,1)S(1)} %add_convert_fusion), channel_id=1, source_target_pairs={{0,48},{48,96},{96,144},{144,192},{192,240},{240,288},{288,336},{3... | collective-permute-start | bytes 786440 | tf_op jit(solution)/shard_map/ppermute | solution.py:41
  168.0 0.7 fusion.31
  168.7 0.0 copy-done.3
  168.7 0.8 maximum_bitcast_fusion
  169.6 1.7 %collective-permute-done.1 = bf16[64,2048]{1,0:T(8,128)(2,1)S(1)} collective-permute-done((bf16[64,2048]{1,0:T(8,128)(2,1)S(1)}, bf16[64,2048]{1,0:T(8,128)(2,1)S(1)}, u32[]{:S(2)}, u32[]{:S(2)}) %collective-permute-start.1) | collective-permute-done | bytes 262176 | tf_op jit(solution)/shard_map/ppermute | solution.py:41
  171.3 0.0 copy-done.4
  171.4 0.9 select_select_fusion
  (5 shorter events, 0.1 us)
Async XLA Ops:
  0.6 44.8 %copy-start = (bf16[1,512,2048]{2,1,0:T(8,128)(2,1)S(1)}, bf16[1,512,2048]{2,1,0:T(8,128)(2,1)}, u32[]{:S(2)}) copy-start(bf16[1,512,2048]{2,1,0:T(8,128)(2,1)} %param.13) | copy-start | bytes 6291460
  5.1 31.9 %copy-start.5 = (f32[1,2048]{1,0:T(1,128)S(1)}, f32[1,2048]{1,0:T(1,128)}, u32[]{:S(2)}) copy-start(f32[1,2048]{1,0:T(1,128)} %param.11) | copy-start | bytes 24580
  5.1 31.9 %copy-start.6 = (f32[1,2048]{1,0:T(1,128)S(1)}, f32[1,2048]{1,0:T(1,128)}, u32[]{:S(2)}) copy-start(f32[1,2048]{1,0:T(1,128)} %param.10) | copy-start | bytes 24580
  5.1 32.4 %copy-start.7 = (bf16[1,2048,1536]{2,1,0:T(8,128)(2,1)S(1)}, bf16[1,2048,1536]{2,1,0:T(8,128)(2,1)}, u32[]{:S(2)}) copy-start(bf16[1,2048,1536]{2,1,0:T(8,128)(2,1)} %param.12) | copy-start | bytes 18874372
  46.1 28.1 %copy-start.1 = (bf16[1,2,64,2048]{3,2,1,0:T(8,128)(2,1)S(1)}, bf16[1,2,64,2048]{3,2,1,0:T(8,128)(2,1)}, u32[]{:S(2)}) copy-start(bf16[1,2,64,2048]{3,2,1,0:T(8,128)(2,1)} %param.7) | copy-start | bytes 1572868
  74.3 9.8 %collective-permute-start = (bf16[64,2048]{1,0:T(8,128)(2,1)S(1)}, bf16[64,2048]{1,0:T(8,128)(2,1)}, u32[]{:S(2)}, u32[]{:S(2)}) collective-permute-start(bf16[64,2048]{1,0:T(8,128)(2,1)S(1)} %add_convert_fusion.1), channel_id=1, source_target_pairs={{0,48},{48,96},{96,144},{144,192},{192,240},{240,288},{288,336},{3... | collective-permute-start | bytes 786440 | tf_op jit(solution)/shard_map/ppermute | solution.py:41
  85.8 26.6 %copy-start.2 = (bf16[64,2048]{1,0:T(8,128)(2,1)}, bf16[64,2048]{1,0:T(8,128)(2,1)S(1)}, u32[]{:S(2)}) copy-start(bf16[64,2048]{1,0:T(8,128)(2,1)S(1)} %fusion.32) | copy-start | bytes 786436
  130.5 30.4 %all-to-all-start.3 = ((bf16[4,64,2048]{2,1,0:T(8,128)(2,1)}), bf16[4,64,2048]{2,1,0:T(8,128)(2,1)}, u32[]{:S(2)}, u32[]{:S(2)}) async-start(bf16[4,64,2048]{2,1,0:T(8,128)(2,1)} %bitcast.102), calls=%async_computation.3 | async-start | bytes 2097152 | tf_op jit(solution)/shard_map/all_to_all | solution.py:34
  136.1 32.6 %copy-start.3 = (bf16[1,64,2048]{2,1,0:T(8,128)(2,1)S(1)}, bf16[1,64,2048]{2,1,0:T(8,128)(2,1)}, u32[]{:S(2)}) copy-start(bf16[1,64,2048]{2,1,0:T(8,128)(2,1)} %fusion.30) | copy-start | bytes 786436
  162.3 9.0 %copy-start.4 = (bf16[2,64,2048]{2,1,0:T(8,128)(2,1)S(1)}, bf16[2,64,2048]{2,1,0:T(8,128)(2,1)}, u32[]{:S(2)}) copy-start(bf16[2,64,2048]{2,1,0:T(8,128)(2,1)} %param.8) | copy-start | bytes 1572868
  163.4 7.9 %collective-permute-start.1 = (bf16[64,2048]{1,0:T(8,128)(2,1)S(1)}, bf16[64,2048]{1,0:T(8,128)(2,1)S(1)}, u32[]{:S(2)}, u32[]{:S(2)}) collective-permute-start(bf16[64,2048]{1,0:T(8,128)(2,1)S(1)} %add_convert_fusion), channel_id=1, source_target_pairs={{0,48},{48,96},{96,144},{144,192},{192,240},{240,288},{288,336},{3... | collective-permute-start | bytes 786440 | tf_op jit(solution)/shard_map/ppermute | solution.py:41
where the time goes:
time: 175 us; the launch traced here: 172 us
  blocking collectives  85.3 us (49%)
  waiting for transfers between devices  26.7 us (15%)
  matrix products  22.1 us (13%)
  starting transfers between devices  15.3 us (9%)
  other arithmetic  11.2 us (6%)
  local copies, waits for them, and re-layouts  7.01 us (4%)
  between operations  4.67 us (3%)
    all_to_all x2, blocking collectives, from_everyone(): lax.all_to_all(jnp.broadcast_to(array[None], (length, *array.shape)), axi...  57.4 us
    all_to_all x1, blocking collectives, summed_on_arrival(): lax.all_to_all(split_up(array, dim, length), axis, 0, 0, tiled=True)  27.9 us
    all_to_all x1, waiting for transfers between devices, summed_on_arrival(): lax.all_to_all(split_up(array, dim, length), axis, 0, 0, tiled=True)  24.8 us
    ppermute x2, starting transfers between devices, from_behind(): return lax.ppermute(block, axis, route)  11.1 us
    dot_general x2, matrix products, body(): jnp.dot(normed(gathered_copies(current, 'tensor', 0), gain, bias), w_in,...  8.12 us
    dot_general x2, matrix products, attend(): jnp.einsum('hqk,khe->qhe', probs, grid[:, :, 2], preferred_element_type=j...  4.74 us
    all_to_all x1, starting transfers between devices, summed_on_arrival(): lax.all_to_all(split_up(array, dim, length), axis, 0, 0, tiled=True)  4.23 us
    convert_element_type x2, local copies, waits for them, and re-layouts, body(): qkv = jnp.dot(normed(gathered_copies(current, 'tensor', 0), gain, bias),...  3.73 us
  transfers between devices with their start and end apart: 3, of which 3 were waited for; matrix products, arithmetic and copies ran while one was open for 2% of the time, Pallas kernels for 0%

commit v1 on v0

v1 whole, which is shorter than its diff:
```python
import functools
import math

import jax
import jax.numpy as jnp
from jax import lax
from jax.experimental import pallas as pl
from jax.experimental.pallas import tpu as pltpu
from jax.sharding import PartitionSpec as P

HD = 128
TICKS = 2
CHUNKS = 4
MESH = pl.DeviceIdType.MESH


def kernel(
    S, T, order, acts_hbm, fresh_hbm, gain, bias, wq_hbm, wo_hbm, out, held,
    acts, wq, wo, xa, norm, qkv, attn, part, from_left, from_right, res, hop,
    acts_sem, wq_sem, wo_sem, ag_recv, ag_right, ag_left,
    rl_recv, rr_recv, rs_right, rs_left, hop_recv, hop_send,
):
    C = CHUNKS
    rows, D = xa.shape[3], xa.shape[4]
    group = T * rows
    local_heads = qkv.shape[1] // (3 * HD)
    p = lax.axis_index("tensor")
    s = lax.axis_index("section")
    last = T - 1

    barrier = pltpu.get_barrier_semaphore()
    links = ((p > 0, {"tensor": p - 1}), (p < last, {"tensor": p + 1}),
             (s > 0, {"section": s - 1}), (s < S - 1, {"section": s + 1}))
    for there, device in links:
        @pl.when(there)
        def _():
            pl.semaphore_signal(barrier, inc=1, device_id=device, device_id_type=MESH)

    acts_in = pltpu.make_async_copy(acts_hbm, acts, acts_sem)
    acts_in.start()
    wq_in = pltpu.make_async_copy(wq_hbm, wq, wq_sem)
    wq_in.start()
    wo_in = pltpu.make_async_copy(wo_hbm, wo, wo_sem)
    wo_in.start()

    @pl.when(s == 0)
    def _():
        for t in range(TICKS):
            for c in range(C):
                pltpu.make_async_copy(fresh_hbm.at[t, c], hop.at[t, c], hop_recv.at[t, c]).start()

    @pl.when(p == 0)
    def _():
        for t in range(TICKS):
            for c in range(C):
                from_left[t, c, 0] = jnp.zeros((rows, D), jnp.bfloat16)

    @pl.when(p == last)
    def _():
        for t in range(TICKS):
            for c in range(C):
                from_right[t, c, last] = jnp.zeros((rows, D), jnp.bfloat16)

    first, second = order[0], order[1]

    def gather_copy(t, c, b, right):
        sem = ag_right if right else ag_left
        return pltpu.make_async_remote_copy(
            src_ref=xa.at[t, c, b], dst_ref=xa.at[t, c, b],
            send_sem=sem.at[t, c, b], recv_sem=ag_recv.at[t, c, b],
            device_id={"tensor": p + 1 if right else p - 1}, device_id_type=MESH)

    def sum_copy(t, c, d, right):
        return pltpu.make_async_remote_copy(
            src_ref=part.at[t, c, d], dst_ref=(from_left if right else from_right).at[t, c, d],
            send_sem=(rs_right if right else rs_left).at[t, c, d],
            recv_sem=(rl_recv if right else rr_recv).at[t, c, d],
            device_id={"tensor": p + 1 if right else p - 1}, device_id_type=MESH)

    def hop_copy(t, c):
        return pltpu.make_async_remote_copy(
            src_ref=res.at[t, c], dst_ref=hop.at[t, c],
            send_sem=hop_send.at[t, c], recv_sem=hop_recv.at[t, c],
            device_id={"section": s + 1}, device_id_type=MESH)

    def gather_own(t, c):
        @pl.when(p < last)
        def _():
            gather_copy(t, c, p, True).start()

        @pl.when(p > 0)
        def _():
            gather_copy(t, c, p, False).start()

    def gather_step(t, c, j):
        b_left, b_right = p - 1 - j, p + 1 + j

        @pl.when(b_left >= 0)
        def _():
            copy = gather_copy(t, c, b_left, True)
            copy.wait_recv()

            @pl.when(p < last)
            def _():
                copy.start()

        @pl.when(b_right <= last)
        def _():
            copy = gather_copy(t, c, b_right, False)
            copy.wait_recv()

            @pl.when(p > 0)
            def _():
                copy.start()

    def project(t, c):
        for b in range(T):
            values = xa[t, c, b].astype(jnp.float32)
            centred = values - jnp.mean(values, axis=-1, keepdims=True)
            spread = jnp.mean(centred * centred, axis=-1, keepdims=True)
            norm[pl.ds(b * rows, rows), :] = (
                centred * lax.rsqrt(spread + 1e-06) * gain[...] + bias[...]
            ).astype(jnp.bfloat16)
        width = math.gcd(256, qkv.shape[1])
        r0 = pl.multiple_of(c * group, group)

        @pl.loop(0, qkv.shape[1] // width)
        def _(n):
            cols = pl.ds(pl.multiple_of(n * width, width), width)
            qkv[pl.ds(r0, group), cols] = jnp.dot(
                norm[...], wq[:, cols], preferred_element_type=jnp.float32
            ).astype(jnp.bfloat16)

    def attend(t, c):
        r0 = pl.multiple_of(c * group, group)
        for h in range(local_heads):
            at = h * 3 * HD
            q = qkv[pl.ds(r0, group), at:at + HD]
            k = qkv[:, at + HD:at + 2 * HD]
            v = qkv[:, at + 2 * HD:at + 3 * HD]
            scores = lax.dot_general(
                q, k, (((1,), (1,)), ((), ())), preferred_element_type=jnp.float32
            ) * (1.0 / math.sqrt(HD))
            top = jnp.max(scores, axis=-1, keepdims=True)
            e = jnp.exp(scores - top)
            probs = (e * (1.0 / jnp.sum(e, axis=-1, keepdims=True))).astype(jnp.bfloat16)
            attn[:, h * HD:(h + 1) * HD] = jnp.dot(
                probs, v, preferred_element_type=jnp.float32
            ).astype(jnp.bfloat16)
        width = min(512, D)
        for n in range(D // width):
            cols = slice(n * width, (n + 1) * width)
            block = jnp.dot(attn[...], wo[:, cols], preferred_element_type=jnp.float32)
            part[t, c, :, :, cols] = block.astype(jnp.bfloat16).reshape(T, rows, width)

        @pl.when(p == 0)
        def _():
            for d in range(last, 0, -1):
                sum_copy(t, c, d, True).start()

        @pl.when(p == last)
        def _():
            for d in range(last):
                sum_copy(t, c, d, False).start()

    def pass_sum(t, c, d, right):
        copy = sum_copy(t, c, d, right)
        copy.wait_recv()
        came = from_left if right else from_right
        part[t, c, d] = (
            part[t, c, d].astype(jnp.float32) + came[t, c, d].astype(jnp.float32)
        ).astype(jnp.bfloat16)
        copy.start()

    def reduce_step(t, c):
        half = T // 2
        for i in range(last):
            up, down = last - i, i

            @pl.when((p > 0) & (p < up) & (p < half))
            def _():
                pass_sum(t, c, up, True)

            @pl.when((p < last) & (p > down))
            def _():
                pass_sum(t, c, down, False)

            @pl.when((p < up) & (p >= half))
            def _():
                pass_sum(t, c, up, True)

        @pl.when(p > 0)
        def _():
            sum_copy(t, c, p, True).wait_recv()

        @pl.when(p < last)
        def _():
            sum_copy(t, c, p, False).wait_recv()
        total = (part[t, c, p].astype(jnp.float32) + from_left[t, c, p].astype(jnp.float32)
                 + from_right[t, c, p].astype(jnp.float32))
        result = (xa[t, c, p].astype(jnp.float32) + total).astype(jnp.bfloat16)
        res[t, c] = result
        out[t, c] = result

        @pl.when(s < S - 1)
        def _():
            hop_copy(t, c).start()

    def arrived(t, c):
        pltpu.make_async_copy(fresh_hbm.at[t, c], hop.at[t, c], hop_recv.at[t, c]).wait()

    acts_in.wait()
    for c in range(C):
        xa[0, c, p] = acts[first, c]
    pl.semaphore_wait(barrier, sum(there.astype(jnp.int32) for there, _ in links))
    for c in range(C):
        gather_own(0, c)
    for j in range(last - 1):
        for c in range(C):
            gather_step(0, c, j)
    wq_in.wait()
    for c in range(C):
        gather_step(0, c, last - 1)
        project(0, c)
    wo_in.wait()

    @pl.loop(0, C)
    def _(c):
        attend(0, c)

    for slot in range(C + last + 1):
        if slot < C:
            reduce_step(0, slot)
        c = slot - 1
        if 0 <= c < C:
            arrived(0, c)
            xa[1, c, p] = jnp.where(first == second, hop[0, c], acts[second, c])
            gather_own(1, c)
        for j in range(last):
            c = slot - 2 - j
            if 0 <= c < C:
                gather_step(1, c, j)
        c = slot - 1 - last
        if 0 <= c < C:
            project(1, c)

    @pl.loop(0, C)
    def _(c):
        attend(1, c)

    for c in range(C):
        reduce_step(1, c)
    for c in range(C):
        arrived(1, c)
        for j in range(2):
            held[j, c] = jnp.where(
                second == j, hop[1, c], jnp.where(first == j, hop[0, c], acts[j, c]))

    for t in range(TICKS):
        @pl.loop(0, C)
        def _(c):
            for b in range(T):
                @pl.when((p < last) & (p >= b))
                def _():
                    gather_copy(t, c, b, True).wait_send()

                @pl.when((p > 0) & (p <= b))
                def _():
                    gather_copy(t, c, b, False).wait_send()

                @pl.when(p < b)
                def _():
                    sum_copy(t, c, b, True).wait_send()

                @pl.when(p > b)
                def _():
                    sum_copy(t, c, b, False).wait_send()

            @pl.when(s < S - 1)
            def _():
                hop_copy(t, c).wait_send()


def body(acts, fresh, order, ln_gain, ln_bias, wqkv, wo):
    S, T = lax.axis_size("section"), lax.axis_size("tensor")
    slots, tokens, D = acts.shape[1:]
    rows = tokens // CHUNKS
    cols = wqkv.shape[2]
    vmem = pl.BlockSpec(memory_space=pltpu.VMEM)
    hbm = pl.BlockSpec(memory_space=pl.ANY)
    block = (TICKS, CHUNKS, rows, D)
    wide = (TICKS, CHUNKS, T, rows, D)
    sem = lambda *shape: pltpu.SemaphoreType.DMA(shape)
    out, held = pl.pallas_call(
        functools.partial(kernel, S, T),
        name="relay",
        out_shape=(jax.ShapeDtypeStruct(block, jnp.bfloat16),) * 2,
        in_specs=[pl.BlockSpec(memory_space=pltpu.SMEM), hbm, hbm, vmem, vmem, hbm, hbm],
        out_specs=(vmem, vmem),
        scratch_shapes=[
            pltpu.VMEM(block, jnp.bfloat16),
            pltpu.VMEM((D, cols), jnp.bfloat16),
            pltpu.VMEM(wo.shape[1:], jnp.bfloat16),
            pltpu.VMEM(wide, jnp.bfloat16),
            pltpu.VMEM((T * rows, D), jnp.bfloat16),
            pltpu.VMEM((T * tokens, cols), jnp.bfloat16),
            pltpu.VMEM((T * rows, cols // 3), jnp.bfloat16),
            pltpu.VMEM(wide, jnp.bfloat16),
            pltpu.VMEM(wide, jnp.bfloat16),
            pltpu.VMEM(wide, jnp.bfloat16),
            pltpu.VMEM(block, jnp.bfloat16),
            pltpu.VMEM(block, jnp.bfloat16),
            pltpu.SemaphoreType.DMA, pltpu.SemaphoreType.DMA, pltpu.SemaphoreType.DMA,
            sem(TICKS, CHUNKS, T), sem(TICKS, CHUNKS, T), sem(TICKS, CHUNKS, T),
            sem(TICKS, CHUNKS, T), sem(TICKS, CHUNKS, T),
            sem(TICKS, CHUNKS, T), sem(TICKS, CHUNKS, T),
            sem(TICKS, CHUNKS), sem(TICKS, CHUNKS),
        ],
        compiler_params=pltpu.CompilerParams(collective_id=0, has_side_effects=True),
    )(
        order[0], acts.reshape(slots, CHUNKS, rows, D), fresh.reshape(TICKS, CHUNKS, rows, D),
        ln_gain, ln_bias, wqkv[0], wo[0],
    )
    return out.reshape(TICKS, 1, tokens, D), held.reshape(1, slots, tokens, D)


def solution(mesh):
    return jax.shard_map(
        body,
        mesh=mesh,
        in_specs=(
            P("section", "dp", "tensor", None),
            P("dp", "tensor", None),
            P("section", None),
            P("section", None),
            P("section", None),
            P("section", None, "tensor"),
            P("section", "tensor", None),
        ),
        out_specs=(P("dp", "section", "tensor", None), P("section", "dp", "tensor", None)),
        check_vma=False,
    )
```

time: 175 us -> 130 us (0.74); the launches traced: 172 us -> 130 us
  Pallas kernels: 0 us -> 125 us
  blocking collectives: 85.3 us -> 0 us
  waiting for transfers between devices: 26.7 us -> 0 us
  matrix products: 22.1 us -> 0 us
  starting transfers between devices: 15.3 us -> 0 us
  other arithmetic: 11.2 us -> 0 us
  between operations: 4.67 us -> 0.64 us
  local copies, waits for them, and re-layouts: 7.01 us -> 3.76 us
    pallas_call x0 -> x1, Pallas kernels: none -> 125 us  [body(): pl.pallas_call(functools.partial(kernel, S, T), name='relay', out_shape=(...]
    all_to_all x3 -> x0, blocking collectives: 85.3 us -> none  [the longest x2 57.4 us: from_everyone(): lax.all_to_all(jnp.broadcast_to(array[None], (length, *array.shape)), axi...]
    all_to_all x1 -> x0, waiting for transfers between devices: 24.8 us -> none  [summed_on_arrival(): lax.all_to_all(split_up(array, dim, length), axis, 0, 0, tiled=True)]
    dot_general x8 -> x0, matrix products: 20 us -> none  [the longest x2 8.12 us: body(): jnp.dot(normed(gathered_copies(current, 'tensor', 0), gain, bias), w_in,...]
    ppermute x2 -> x0, starting transfers between devices: 11.1 us -> none  [from_behind(): return lax.ppermute(block, axis, route)]
    all_to_all x1 -> x0, starting transfers between devices: 4.23 us -> none  [summed_on_arrival(): lax.all_to_all(split_up(array, dim, length), axis, 0, 0, tiled=True)]
    convert_element_type x2 -> x0, local copies, waits for them, and re-layouts: 3.73 us -> none  [body(): qkv = jnp.dot(normed(gathered_copies(current, 'tensor', 0), gain, bias),...]
    unnamed x16 -> x2, local copies, waits for them, and re-layouts: 0.05 us -> 3.76 us
  transfers between devices with their start and end apart: 3 -> 0, of which waited for: 3 -> 0; matrix products, arithmetic and copies ran while one was open for 2% -> 0% of each run, Pallas kernels for 0% -> 0%
where the time goes in v1:
time: 130 us
  Pallas kernels  125 us (96%)
  local copies, waits for them, and re-layouts  3.76 us (3%)
    pallas_call x1, Pallas kernels, body(): pl.pallas_call(functools.partial(kernel, S, T), name='relay', out_shape=(...  125 us
    unnamed x2, local copies, waits for them, and re-layouts  3.76 us

profile of v1, /device:TPU:1, one launch (start us, length us, event | category | flops | bytes accessed | tf_op | source)
XLA Modules:
  0.0 129.9 jit_solution(10511407631668955188)
XLA Ops:
  0.6 125.5 %relay.1 = (bf16[2,4,16,2048]{3,2,1,0:T(8,128)(2,1)}, bf16[2,4,16,2048]{3,2,1,0:T(8,128)(2,1)}) custom-call(s32[2]{0:T(128)} %bitcast.15, bf16[2,4,16,2048]{3,2,1,0:T(8,128)(2,1)} %bitcast.11, bf16[2,4,16,2048]{3,2,1,0:T(8,128)(2,1)} %bitcast.12, f32[1,2048]{1,0:T(1,128)} %gain.1, f32[1,2048]{1,0:T(1,128)} %bias.1, bf16[2048,1536]{1,0:T(8,128)(2,1)} %bitcast.9, ...), custom_call_target="tpu_custom_call" | custom-call | tf_op jit(solution)/shard_map/relay/pallas_call | solution.py:294
  126.1 1.9 %copy.12 = bf16[2,1,64,2048]{3,2,1,0:T(8,128)(2,1)} copy(bf16[2,1,64,2048]{3,2,1,0:T(8,128)(2,1)} %bitcast.14) | data formatting | bytes 1048576
  128.0 1.9 %copy.13 = bf16[1,2,64,2048]{3,2,1,0:T(8,128)(2,1)} copy(bf16[1,2,64,2048]{3,2,1,0:T(8,128)(2,1)} %bitcast.13) | data formatting | bytes 1048576

commit v2 on v1

v2 whole, which is shorter than its diff:
```python
import functools
import math

import jax
import jax.numpy as jnp
from jax import lax
from jax.experimental import pallas as pl
from jax.experimental.pallas import tpu as pltpu
from jax.sharding import PartitionSpec as P

HD = 128
TICKS = 2
CHUNKS = 8
ATTEND = 2
PROJECT = 4
MESH = pl.DeviceIdType.MESH


def plan(T, C, steps, queue):
    last, per = T - 1, C // steps
    wire, reach, hop_wire, hop_reach = 5.64 / C, 2.2, 2.82 / C, 2.6
    add, norm, attend, project = 0.5 / C, 0.8 / C, 1.0, 2.0
    clock, free, arrivals = [0.0] * T, {}, {}

    def send(link, key, at, wire=wire, reach=reach):
        free[link] = max(at, free.get(link, 0.0)) + wire
        arrivals[key] = free[link] + reach

    orders = []
    for t in range(TICKS):
        for p in range(T):
            for k in range(steps):
                clock[p] += attend
                for q, (c, d) in queue(t, k):
                    if p == q:
                        send((p, d > p), ("sum", t, p + 1 if d > p else p - 1, c, d, d > p), clock[p])
        todo, order = [], [[] for _ in range(T)]
        for p in range(T):
            todo.append([("up", c, d) for c in range(C) for d in range(p + 1, T) if p > 0]
                        + [("down", c, d) for c in range(C) for d in range(p) if p < last]
                        + [("own", c, p) for c in range(C)] + [("next", c, p) for c in range(C)])
            if t == 0:
                todo[p] += [("left", c, b) for c in range(C) for b in range(p)]
                todo[p] += [("right", c, b) for c in range(C) for b in range(p + 1, T)]
                todo[p] += [("project", k, p) for k in range(C // PROJECT)]
        sums = ("up", "down", "own")
        rank = {"up": 0, "down": 0, "own": 1, "next": 2, "left": 3, "right": 3, "project": 4}

        def ready(p, kind, c, d):
            need = []
            if kind == "up" or (kind == "own" and p > 0):
                need.append(("sum", t, p, c, d, True))
            if kind == "down" or (kind == "own" and p < last):
                need.append(("sum", t, p, c, d, False))
            if kind == "next":
                need.append(("hop", t, p, c))
                if c == C - 1 and any(e[0] in sums for e in todo[p]):
                    return None
            if kind in ("left", "right"):
                need.append(("gather", p, c, d))
            if kind == "project" and any(
                    e[0] in ("next", "left", "right") and e[1] // PROJECT == c for e in todo[p]):
                return None
            times = [arrivals.get(key) for key in need]
            return None if None in times else max([clock[p]] + times)

        while any(todo):
            at, _, c, p, (kind, c, d) = min(
                (ready(p, *e), rank[e[0]], e[1], p, e)
                for p in range(T) for e in todo[p] if ready(p, *e) is not None)
            todo[p].remove((kind, c, d))
            order[p].append((kind, c, d))
            if kind in ("up", "down"):
                up = kind == "up"
                at += add
                send((p, up), ("sum", t, p + 1 if up else p - 1, c, d, up), at)
            elif kind == "own":
                at += add
                send((p, "hop"), ("hop", t, p, c), at, hop_wire, hop_reach)
            elif kind == "project":
                at += project
            elif t == 0:
                if kind in ("next", "left") and p < last:
                    send((p, True), ("gather", p + 1, c, d), at)
                if kind in ("next", "right") and p > 0:
                    send((p, False), ("gather", p - 1, c, d), at)
                at += norm
            clock[p] = at
        orders.append(order)
    return orders


def edge_queue(T, C, steps):
    last, per = T - 1, C // steps

    def queue(t, k):
        ends = [(0, list(range(last, 0, -1))), (last, list(range(last)))]
        sends = [(p, (c, far[0])) for p, far in ends for c in range(k * per, (k + 1) * per)]
        if k == steps - 1:
            for p, far in ends:
                rest = [(c, d) for c in range(C) for d in far[1:]]
                if t == TICKS - 1:
                    rest = [(c, d) for d in far[1:] for c in range(C)]
                sends += [(p, e) for e in rest]
        return sends

    return queue


def kernel(
    S, T, order_hbm, acts_hbm, fresh_hbm, gain_hbm, bias_hbm, wq_hbm, wo_hbm, out, held,
    order, acts, gain, bias, wq, wo, xa, norm, qkv, attn, part, from_left, from_right, res, hop,
    order_sem, acts_sem, gain_sem, bias_sem, wq_sem, wo_sem, ag_recv, rl_recv, rr_recv,
    sent_right, sent_left, hop_recv, hop_sent,
):
    C = CHUNKS
    rows, D = xa.shape[3], xa.shape[4]
    group = T * rows
    local_heads = qkv.shape[1] // (3 * HD)
    p = lax.axis_index("tensor")
    s = lax.axis_index("section")
    last = T - 1
    steps = C // ATTEND
    per = ATTEND
    queue = edge_queue(T, C, steps)
    orders = plan(T, C, steps, queue)

    barrier = pltpu.get_barrier_semaphore()
    links = ((p > 0, {"tensor": p - 1}), (p < last, {"tensor": p + 1}),
             (s > 0, {"section": s - 1}), (s < S - 1, {"section": s + 1}))
    for there, device in links:
        @pl.when(there)
        def _():
            pl.semaphore_signal(barrier, inc=1, device_id=device, device_id_type=MESH)

    order_in = pltpu.make_async_copy(order_hbm, order, order_sem)
    acts_in = pltpu.make_async_copy(acts_hbm, acts, acts_sem)
    gain_in = pltpu.make_async_copy(gain_hbm, gain, gain_sem)
    bias_in = pltpu.make_async_copy(bias_hbm, bias, bias_sem)
    wq_in = pltpu.make_async_copy(wq_hbm, wq, wq_sem)
    wo_in = pltpu.make_async_copy(wo_hbm, wo, wo_sem)
    for copy in (order_in, acts_in, gain_in, bias_in, wq_in, wo_in):
        copy.start()

    @pl.when(s == 0)
    def _():
        for t in range(TICKS):
            for c in range(C):
                pltpu.make_async_copy(fresh_hbm.at[t, c], hop.at[t, c], hop_recv.at[t, c]).start()

    def scoped(name):
        return lambda f: jax.named_scope(name)(f)

    def gather_copy(t, c, b, right):
        return pltpu.make_async_remote_copy(
            src_ref=xa.at[t, c, b], dst_ref=xa.at[t, c, b],
            send_sem=(sent_right if right else sent_left).at[t], recv_sem=ag_recv.at[t, c, b],
            device_id={"tensor": p + 1 if right else p - 1}, device_id_type=MESH)

    def sum_copy(t, c, d, right):
        return pltpu.make_async_remote_copy(
            src_ref=part.at[t, c, d], dst_ref=(from_left if right else from_right).at[t, c, d],
            send_sem=(sent_right if right else sent_left).at[t],
            recv_sem=(rl_recv if right else rr_recv).at[c, d],
            device_id={"tensor": p + 1 if right else p - 1}, device_id_type=MESH)

    def hop_copy(t, c):
        return pltpu.make_async_remote_copy(
            src_ref=res.at[t, c], dst_ref=hop.at[t, c],
            send_sem=hop_sent.at[t], recv_sem=hop_recv.at[t, c],
            device_id={"section": s + 1}, device_id_type=MESH)

    @scoped("gather_own")
    def gather_own(t, c):
        @pl.when(p < last)
        def _():
            gather_copy(t, c, p, True).start()

        @pl.when(p > 0)
        def _():
            gather_copy(t, c, p, False).start()

    @scoped("normed")
    def normed(t, c, b):
        values = xa[t, c, b].astype(jnp.float32)
        centred = values - jnp.mean(values, axis=-1, keepdims=True)
        spread = jnp.mean(centred * centred, axis=-1, keepdims=True)
        norm[c, b] = (
            centred * lax.rsqrt(spread + 1e-06) * gain[...] + bias[...]
        ).astype(jnp.bfloat16)

    @scoped("gather_step")
    def gather_step(t, c, j):
        b_left, b_right = p - 1 - j, p + 1 + j

        @pl.when(b_left >= 0)
        def _():
            copy = gather_copy(t, c, b_left, True)
            copy.wait_recv()

            @pl.when(p < last)
            def _():
                copy.start()

        @pl.when(b_right <= last)
        def _():
            copy = gather_copy(t, c, b_right, False)
            copy.wait_recv()

            @pl.when(p > 0)
            def _():
                copy.start()

        @pl.when(b_left >= 0)
        def _():
            normed(t, c, b_left)

        @pl.when(b_right <= last)
        def _():
            normed(t, c, b_right)

    @scoped("project")
    def project(part_of):
        width = math.gcd(256, qkv.shape[1])
        span = PROJECT * group

        @pl.loop(0, qkv.shape[1] // width)
        def _(n):
            cols = pl.ds(pl.multiple_of(n * width, width), width)
            qkv[part_of * span:(part_of + 1) * span, cols] = jnp.dot(
                norm[PROJECT * part_of:PROJECT * (part_of + 1)].reshape(span, D), wq[:, cols],
                preferred_element_type=jnp.float32,
            ).astype(jnp.bfloat16)

    @scoped("attend")
    def attend(t, part_of):
        span = ATTEND * group
        r0 = pl.multiple_of(part_of * span, span)
        heads = range(local_heads)

        def columns(h, j):
            return slice((h * 3 + j) * HD, (h * 3 + j + 1) * HD)

        scores = [lax.dot_general(
            qkv[pl.ds(r0, span), columns(h, 0)], qkv[:, columns(h, 1)],
            (((1,), (1,)), ((), ())), preferred_element_type=jnp.float32) for h in heads]
        scores = [x * (1.0 / math.sqrt(HD)) for x in scores]
        tops = [jnp.max(x, axis=-1, keepdims=True) for x in scores]
        powers = [jnp.exp(x - top) for x, top in zip(scores, tops)]
        sums = [jnp.sum(x, axis=-1, keepdims=True) for x in powers]
        probs = [(x * (1.0 / total)).astype(jnp.bfloat16) for x, total in zip(powers, sums)]
        mixed = [jnp.dot(probs[h], qkv[:, columns(h, 2)], preferred_element_type=jnp.float32)
                 for h in heads]
        for h in heads:
            attn[:, h * HD:(h + 1) * HD] = mixed[h].astype(jnp.bfloat16)
        width = min(512, D)
        for n in range(D // width):
            cols = slice(n * width, (n + 1) * width)
            block = jnp.dot(attn[...], wo[:, cols], preferred_element_type=jnp.float32)
            block = block.reshape(ATTEND, T, rows, width).astype(jnp.bfloat16)
            part[t, pl.ds(part_of * ATTEND, ATTEND), :, :, cols] = block
        for c in range(ATTEND):
            c += part_of * ATTEND

            @pl.when(p == 0)
            def _():
                sum_copy(t, c, last, True).start()

            @pl.when(p == last)
            def _():
                sum_copy(t, c, 0, False).start()

    def send_rest(t):
        for q in (0, last):
            @pl.when(p == q)
            def _():
                for end, (c, d) in queue(t, steps - 1)[2 * per:]:
                    if end == q:
                        sum_copy(t, c, d, q == 0).start()

    def pass_sum(t, c, d, right):
        copy = sum_copy(t, c, d, right)
        copy.wait_recv()
        came = from_left if right else from_right
        part[t, c, d] = (
            part[t, c, d].astype(jnp.float32) + came[t, c, d].astype(jnp.float32)
        ).astype(jnp.bfloat16)
        copy.start()

    @scoped("sum_own")
    def sum_own(t, c, q):
        total = part[t, c, q].astype(jnp.float32)
        if q > 0:
            sum_copy(t, c, q, True).wait_recv()
            total += from_left[t, c, q].astype(jnp.float32)
        if q < last:
            sum_copy(t, c, q, False).wait_recv()
            total += from_right[t, c, q].astype(jnp.float32)
        result = (xa[t, c, q].astype(jnp.float32) + total).astype(jnp.bfloat16)
        res[t, c] = result

        @pl.when(s < S - 1)
        def _():
            hop_copy(t, c).start()
        out[t, c] = result

    @scoped("arrived")
    def arrived(t, c):
        pltpu.make_async_copy(fresh_hbm.at[t, c], hop.at[t, c], hop_recv.at[t, c]).wait()

    def drain(t):
        for right, there in ((True, p < last), (False, p > 0)):
            @pl.when(there)
            def _():
                pltpu.make_async_remote_copy(
                    src_ref=xa.at[t], dst_ref=xa.at[t],
                    send_sem=(sent_right if right else sent_left).at[t], recv_sem=ag_recv.at[t, 0, 0],
                    device_id={"tensor": p + 1 if right else p - 1}, device_id_type=MESH,
                ).wait_send()

        @pl.when(s < S - 1)
        def _():
            pltpu.make_async_remote_copy(
                src_ref=res.at[t], dst_ref=hop.at[t],
                send_sem=hop_sent.at[t], recv_sem=hop_recv.at[t, 0],
                device_id={"section": s + 1}, device_id_type=MESH).wait_send()

    def step(t, q, kind, c, d):
        if kind in ("up", "down"):
            with jax.named_scope("pass_sum"):
                pass_sum(t, c, d, kind == "up")
        elif kind == "own":
            sum_own(t, c, q)
        elif kind == "project":
            project(c)
        elif kind == "next" and t == 0:
            arrived(0, c)
            xa[1, c, q] = jnp.where(first == second, hop[0, c], acts[second, c])
            if q < last:
                gather_copy(1, c, q, True).start()
            if q > 0:
                gather_copy(1, c, q, False).start()
            normed(1, c, q)
        elif kind == "next":
            arrived(1, c)
            for j in range(2):
                held[j, c] = jnp.where(
                    second == j, hop[1, c], jnp.where(first == j, hop[0, c], acts[j, c]))
        else:
            with jax.named_scope("gather_step"):
                copy = gather_copy(1, c, d, kind == "left")
                copy.wait_recv()
                if (q < last) if kind == "left" else (q > 0):
                    copy.start()
            normed(1, c, d)

    with jax.named_scope("acts_wait"):
        order_in.wait()
        acts_in.wait()
    first, second = order[0, 0], order[0, 1]
    for c in range(C):
        xa[0, c, p] = acts[first, c]
    with jax.named_scope("entry"):
        pl.semaphore_wait(barrier, sum(there.astype(jnp.int32) for there, _ in links))
    for c in range(C):
        gather_own(0, c)

    gain_in.wait()
    bias_in.wait()
    for c in range(C):
        normed(0, c, p)
    for j in range(last - 1):
        for c in range(C):
            gather_step(0, c, j)
    wq_in.wait()
    for c in range(C):
        gather_step(0, c, last - 1)
        if c % PROJECT == PROJECT - 1:
            project(c // PROJECT)
    wo_in.wait()

    for t in range(TICKS):
        @pl.loop(0, steps)
        def _(part_of):
            attend(t, part_of)

        send_rest(t)
        for q in range(T):
            @pl.when(p == q)
            def _():
                for event in orders[t][q]:
                    step(t, q, *event)
        with jax.named_scope("drain"):
            drain(t)


def store(out, held, out_hbm, held_hbm, out_sem, held_sem):
    copies = (pltpu.make_async_copy(out, out_hbm, out_sem),
              pltpu.make_async_copy(held, held_hbm, held_sem))
    for copy in copies:
        copy.start()
    for copy in copies:
        copy.wait()


def body(acts, fresh, order, ln_gain, ln_bias, wqkv, wo):
    S, T = lax.axis_size("section"), lax.axis_size("tensor")
    slots, tokens, D = acts.shape[1:]
    rows = tokens // CHUNKS
    cols = wqkv.shape[2]
    vmem = pl.BlockSpec(memory_space=pltpu.VMEM)
    hbm = pl.BlockSpec(memory_space=pltpu.HBM)
    block = (TICKS, CHUNKS, rows, D)
    wide = (TICKS, CHUNKS, T, rows, D)
    sem = lambda *shape: pltpu.SemaphoreType.DMA(shape)
    out, held = pl.pallas_call(
        functools.partial(kernel, S, T),
        name="relay",
        out_shape=(jax.ShapeDtypeStruct(block, jnp.bfloat16),) * 2,
        in_specs=[hbm, hbm, hbm, hbm, hbm, hbm, hbm],
        out_specs=(vmem, vmem),
        scratch_shapes=[
            pltpu.SMEM(order.shape, jnp.int32),
            pltpu.VMEM(block, jnp.bfloat16),
            pltpu.VMEM((1, D), jnp.float32),
            pltpu.VMEM((1, D), jnp.float32),
            pltpu.VMEM((D, cols), jnp.bfloat16),
            pltpu.VMEM(wo.shape[1:], jnp.bfloat16),
            pltpu.VMEM(wide, jnp.bfloat16),
            pltpu.VMEM((CHUNKS, T, rows, D), jnp.bfloat16),
            pltpu.VMEM((T * tokens, cols), jnp.bfloat16),
            pltpu.VMEM((ATTEND * T * rows, cols // 3), jnp.bfloat16),
            pltpu.VMEM(wide, jnp.bfloat16),
            pltpu.VMEM(wide, jnp.bfloat16),
            pltpu.VMEM(wide, jnp.bfloat16),
            pltpu.VMEM(block, jnp.bfloat16),
            pltpu.VMEM(block, jnp.bfloat16),
            *[pltpu.SemaphoreType.DMA] * 6,
            sem(TICKS, CHUNKS, T), sem(CHUNKS, T), sem(CHUNKS, T),
            sem(TICKS), sem(TICKS), sem(TICKS, CHUNKS), sem(TICKS),
        ],
        compiler_params=pltpu.CompilerParams(
            collective_id=0, has_side_effects=True, vmem_limit_bytes=32 << 20),
    )(*(pltpu.with_memory_space_constraint(x, pltpu.HBM) for x in (
        order, acts.reshape(slots, CHUNKS, rows, D), fresh.reshape(TICKS, CHUNKS, rows, D),
        ln_gain, ln_bias, wqkv[0], wo[0],
    )))
    out, held = pl.pallas_call(
        store, name="store",
        out_shape=(jax.ShapeDtypeStruct(block, jnp.bfloat16),) * 2,
        in_specs=[vmem, vmem], out_specs=(hbm, hbm),
        scratch_shapes=[pltpu.SemaphoreType.DMA, pltpu.SemaphoreType.DMA],
        compiler_params=pltpu.CompilerParams(vmem_limit_bytes=4 << 20),
    )(out, held)
    return out.reshape(TICKS, 1, tokens, D), held.reshape(1, slots, tokens, D)


def solution(mesh):
    return jax.shard_map(
        body,
        mesh=mesh,
        in_specs=(
            P("section", "dp", "tensor", None),
            P("dp", "tensor", None),
            P("section", None),
            P("section", None),
            P("section", None),
            P("section", None, "tensor"),
            P("section", "tensor", None),
        ),
        out_specs=(P("dp", "section", "tensor", None), P("section", "dp", "tensor", None)),
        check_vma=False,
    )
```

time: 130 us -> 90.4 us (0.70)
  Pallas kernels: 125 us -> 88.7 us
  local copies, waits for them, and re-layouts: 3.76 us -> 0 us
    pallas_call x1, Pallas kernels: 125 us -> 87.7 us  [body(): pl.pallas_call(functools.partial(kernel, S, T), name='relay', out_shape=(...]
    unnamed x2 -> x0, local copies, waits for them, and re-layouts: 3.76 us -> none
where the time goes in v2:
time: 90.4 us; the launch traced here: 89.5 us
  Pallas kernels  88.7 us (98%)
    pallas_call x1, Pallas kernels, body(): pl.pallas_call(functools.partial(kernel, S, T), name='relay', out_shape=(...  87.7 us

profile of v2, /device:TPU:1, one launch (start us, length us, event | category | flops | bytes accessed | tf_op | source)
XLA Modules:
  0.0 89.5 jit_solution(6787280831990012760)
XLA Ops:
  0.6 87.7 %relay.1 = (bf16[2,8,8,2048]{3,2,1,0:T(8,128)(2,1)S(1)}, bf16[2,8,8,2048]{3,2,1,0:T(8,128)(2,1)S(1)}) custom-call(s32[1,2]{1,0:T(1,128)} %order_hbm.1, bf16[2,8,8,2048]{3,2,1,0:T(8,128)(2,1)} %bitcast.10, bf16[2,8,8,2048]{3,2,1,0:T(8,128)(2,1)} %bitcast.11, f32[1,2048]{1,0:T(1,128)} %gain_hbm.1, f32[1,2048]{1,0:T(1,128)} %bias_hbm.1, ...), custom_call_target="tpu_custom_call" | custom-call | tf_op jit(solution)/shard_map/relay/pallas_call | solution.py:416
  88.3 1.0 %store.1 = (bf16[2,8,8,2048]{3,2,1,0:T(8,128)(2,1)}, bf16[2,8,8,2048]{3,2,1,0:T(8,128)(2,1)}) custom-call(bf16[2,8,8,2048]{3,2,1,0:T(8,128)(2,1)S(1)} %get-tuple-element.6.out, bf16[2,8,8,2048]{3,2,1,0:T(8,128)(2,1)S(1)} %get-tuple-element.7.held), custom_call_target="tpu_custom_call" | custom-call | tf_op jit(solution)/shard_map/store/pallas_call | solution.py:448

commit v3 on v2

--- a/solution.py
+++ b/solution.py
@@ -19,7 +19,7 @@
 def plan(T, C, steps, queue):
     last, per = T - 1, C // steps
     wire, reach, hop_wire, hop_reach = 5.64 / C, 2.2, 2.82 / C, 2.6
-    add, norm, attend, project = 0.5 / C, 0.8 / C, 1.0, 2.0
+    add, norm, attend, project = 0.5 / C, 0.8 / C, 1.0, 1.7
     clock, free, arrivals = [0.0] * T, {}, {}
 
     def send(link, key, at, wire=wire, reach=reach):
@@ -92,16 +92,16 @@
 
 def edge_queue(T, C, steps):
     last, per = T - 1, C // steps
+    lead = (0, 5, 7)
 
     def queue(t, k):
-        ends = [(0, list(range(last, 0, -1))), (last, list(range(last)))]
-        sends = [(p, (c, far[0])) for p, far in ends for c in range(k * per, (k + 1) * per)]
-        if k == steps - 1:
-            for p, far in ends:
-                rest = [(c, d) for c in range(C) for d in far[1:]]
-                if t == TICKS - 1:
-                    rest = [(c, d) for d in far[1:] for c in range(C)]
-                sends += [(p, e) for e in rest]
+        turns = [(i, c) if t == TICKS - 1 else (c + lead[i], -i, c) for c in range(C) for i in range(last)]
+        turns = sorted(zip(turns, [(c, i) for c in range(C) for i in range(last)]))
+        at, sends = 0, []
+        for _, (c, i) in turns:
+            at = max(at, c // per)
+            if at == k:
+                sends += [(0, (c, last - i)), (last, (c, i))]
         return sends
 
     return queue
@@ -121,7 +121,6 @@
     s = lax.axis_index("section")
     last = T - 1
     steps = C // ATTEND
-    per = ATTEND
     queue = edge_queue(T, C, steps)
     orders = plan(T, C, steps, queue)
 
@@ -161,7 +160,7 @@
         return pltpu.make_async_remote_copy(
             src_ref=part.at[t, c, d], dst_ref=(from_left if right else from_right).at[t, c, d],
             send_sem=(sent_right if right else sent_left).at[t],
-            recv_sem=(rl_recv if right else rr_recv).at[c, d],
+            recv_sem=rl_recv.at[c, d - 1] if right else rr_recv.at[c, d],
             device_id={"tensor": p + 1 if right else p - 1}, device_id_type=MESH)
 
     def hop_copy(t, c):
@@ -220,17 +219,38 @@
             normed(t, c, b_right)
 
     @scoped("project")
-    def project(part_of):
-        width = math.gcd(256, qkv.shape[1])
+    def project(part_of, begin, width):
         span = PROJECT * group
 
-        @pl.loop(0, qkv.shape[1] // width)
-        def _(n):
-            cols = pl.ds(pl.multiple_of(n * width, width), width)
+        @pl.loop(0, local_heads)
+        def _(h):
+            cols = pl.ds(pl.multiple_of(h * (3 * HD), HD) + begin, width)
             qkv[part_of * span:(part_of + 1) * span, cols] = jnp.dot(
                 norm[PROJECT * part_of:PROJECT * (part_of + 1)].reshape(span, D), wq[:, cols],
                 preferred_element_type=jnp.float32,
             ).astype(jnp.bfloat16)
+
+    def project_keys(part_of):
+        project(part_of, HD, 2 * HD)
+
+    def project_queries(part_of):
+        project(part_of, 0, HD)
+
+    def project_part(part_of):
+        project_keys(part_of)
+        if part_of < C // PROJECT - 1:
+            project_queries(part_of)
+
+    def attend_all(t):
+        half = steps // (C // PROJECT)
+
+        for part in range(C // PROJECT):
+            @pl.loop(part * half, (part + 1) * half)
+            def _(k):
+                attend(t, k)
+
+            if part == C // PROJECT - 2:
+                project_queries(part + 1)
 
     @scoped("attend")
     def attend(t, part_of):
@@ -259,24 +279,13 @@
             block = jnp.dot(attn[...], wo[:, cols], preferred_element_type=jnp.float32)
             block = block.reshape(ATTEND, T, rows, width).astype(jnp.bfloat16)
             part[t, pl.ds(part_of * ATTEND, ATTEND), :, :, cols] = block
-        for c in range(ATTEND):
-            c += part_of * ATTEND
-
-            @pl.when(p == 0)
-            def _():
-                sum_copy(t, c, last, True).start()
-
-            @pl.when(p == last)
-            def _():
-                sum_copy(t, c, 0, False).start()
-
-    def send_rest(t):
-        for q in (0, last):
-            @pl.when(p == q)
-            def _():
-                for end, (c, d) in queue(t, steps - 1)[2 * per:]:
-                    if end == q:
-                        sum_copy(t, c, d, q == 0).start()
+        for k in range(steps):
+            for q in (0, last):
+                @pl.when((part_of == k) & (p == q))
+                def _():
+                    for end, (c, d) in queue(t, k):
+                        if end == q:
+                            sum_copy(t, c, d, q == 0).start()
 
     def pass_sum(t, c, d, right):
         copy = sum_copy(t, c, d, right)
@@ -332,7 +341,7 @@
         elif kind == "own":
             sum_own(t, c, q)
         elif kind == "project":
-            project(c)
+            project_part(c)
         elif kind == "next" and t == 0:
             arrived(0, c)
             xa[1, c, q] = jnp.where(first == second, hop[0, c], acts[second, c])
@@ -376,15 +385,11 @@
     for c in range(C):
         gather_step(0, c, last - 1)
         if c % PROJECT == PROJECT - 1:
-            project(c // PROJECT)
+            project_part(c // PROJECT)
     wo_in.wait()
 
     for t in range(TICKS):
-        @pl.loop(0, steps)
-        def _(part_of):
-            attend(t, part_of)
-
-        send_rest(t)
+        attend_all(t)
         for q in range(T):
             @pl.when(p == q)
             def _():
@@ -436,7 +441,7 @@
             pltpu.VMEM(block, jnp.bfloat16),
             pltpu.VMEM(block, jnp.bfloat16),
             *[pltpu.SemaphoreType.DMA] * 6,
-            sem(TICKS, CHUNKS, T), sem(CHUNKS, T), sem(CHUNKS, T),
+            sem(TICKS, CHUNKS, T), sem(CHUNKS, T - 1), sem(CHUNKS, T - 1),
             sem(TICKS), sem(TICKS), sem(TICKS, CHUNKS), sem(TICKS),
         ],
         compiler_params=pltpu.CompilerParams(

time: 90.4 us -> 89.6 us (level)
  Pallas kernels: 88.7 us -> 87.6 us
    pallas_call x1, Pallas kernels: 87.7 us -> 86.6 us  [body(): pl.pallas_call(functools.partial(kernel, S, T), name='relay', out_shape=(...]
where the time goes in v3:
time: 89.6 us; the launch traced here: 88.4 us
  Pallas kernels  87.6 us (98%)
    pallas_call x1, Pallas kernels, body(): pl.pallas_call(functools.partial(kernel, S, T), name='relay', out_shape=(...  86.6 us

profile of v3, /device:TPU:1, one launch (start us, length us, event | category | flops | bytes accessed | tf_op | source)
XLA Modules:
  0.0 88.4 jit_solution(11988004774991532680)
XLA Ops:
  0.6 86.6 %relay.1 = (bf16[2,8,8,2048]{3,2,1,0:T(8,128)(2,1)S(1)}, bf16[2,8,8,2048]{3,2,1,0:T(8,128)(2,1)S(1)}) custom-call(s32[1,2]{1,0:T(1,128)} %order_hbm.1, bf16[2,8,8,2048]{3,2,1,0:T(8,128)(2,1)} %bitcast.10, bf16[2,8,8,2048]{3,2,1,0:T(8,128)(2,1)} %bitcast.11, f32[1,2048]{1,0:T(1,128)} %gain_hbm.1, f32[1,2048]{1,0:T(1,128)} %bias_hbm.1, ...), custom_call_target="tpu_custom_call" | custom-call | tf_op jit(solution)/shard_map/relay/pallas_call | solution.py:421
  87.2 1.0 %store.1 = (bf16[2,8,8,2048]{3,2,1,0:T(8,128)(2,1)}, bf16[2,8,8,2048]{3,2,1,0:T(8,128)(2,1)}) custom-call(bf16[2,8,8,2048]{3,2,1,0:T(8,128)(2,1)S(1)} %get-tuple-element.6.out, bf16[2,8,8,2048]{3,2,1,0:T(8,128)(2,1)S(1)} %get-tuple-element.7.held), custom_call_target="tpu_custom_call" | custom-call | tf_op jit(solution)/shard_map/store/pallas_call | solution.py:453

commit v4 on v3

--- a/solution.py
+++ b/solution.py
@@ -76,13 +76,17 @@
                 send((p, up), ("sum", t, p + 1 if up else p - 1, c, d, up), at)
             elif kind == "own":
                 at += add
+                if t == 0:
+                    for q in (p - 1, p + 1):
+                        if 0 <= q < T:
+                            send((p, q > p), ("gather", q, c, p), at, reach=reach + 0.7)
                 send((p, "hop"), ("hop", t, p, c), at, hop_wire, hop_reach)
             elif kind == "project":
                 at += project
             elif t == 0:
-                if kind in ("next", "left") and p < last:
+                if kind == "left" and p < last:
                     send((p, True), ("gather", p + 1, c, d), at)
-                if kind in ("next", "right") and p > 0:
+                if kind == "right" and p > 0:
                     send((p, False), ("gather", p - 1, c, d), at)
                 at += norm
             clock[p] = at
@@ -110,8 +114,9 @@
 def kernel(
     S, T, order_hbm, acts_hbm, fresh_hbm, gain_hbm, bias_hbm, wq_hbm, wo_hbm, out, held,
     order, acts, gain, bias, wq, wo, xa, norm, qkv, attn, part, from_left, from_right, res, hop,
-    order_sem, acts_sem, gain_sem, bias_sem, wq_sem, wo_sem, ag_recv, rl_recv, rr_recv,
-    sent_right, sent_left, hop_recv, hop_sent,
+    mine, other, flag, flag_next, chosen,
+    order_sem, acts_sem, gain_sem, bias_sem, wq_sem, wo_sem, ag_first, ag_recv, rl_recv, rr_recv,
+    sent_right, sent_left, hop_first, hop_recv, hop_sent, next_sent, back_recv, back_sent,
 ):
     C = CHUNKS
     rows, D = xa.shape[3], xa.shape[4]
@@ -126,7 +131,9 @@
 
     barrier = pltpu.get_barrier_semaphore()
     links = ((p > 0, {"tensor": p - 1}), (p < last, {"tensor": p + 1}),
-             (s > 0, {"section": s - 1}), (s < S - 1, {"section": s + 1}))
+             (s > 0, {"section": s - 1}), (s < S - 1, {"section": s + 1}),
+             *(((0 <= q) & (q <= last) & (0 <= r) & (r < S), {"section": r, "tensor": q})
+               for q in (p - 1, p + 1) for r in (s - 1, s + 1)))
     for there, device in links:
         @pl.when(there)
         def _():
@@ -143,31 +150,50 @@
 
     @pl.when(s == 0)
     def _():
-        for t in range(TICKS):
-            for c in range(C):
-                pltpu.make_async_copy(fresh_hbm.at[t, c], hop.at[t, c], hop_recv.at[t, c]).start()
+        pltpu.make_async_copy(fresh_hbm.at[0], hop.at[0], hop_first).start()
+        for c in range(C):
+            pltpu.make_async_copy(fresh_hbm.at[1, c], hop.at[1, c], hop_recv.at[c]).start()
 
     def scoped(name):
         return lambda f: jax.named_scope(name)(f)
 
     def gather_copy(t, c, b, right):
+        where = pl.ds(2 * c, 2) if t == 0 else c
         return pltpu.make_async_remote_copy(
-            src_ref=xa.at[t, c, b], dst_ref=xa.at[t, c, b],
-            send_sem=(sent_right if right else sent_left).at[t], recv_sem=ag_recv.at[t, c, b],
+            src_ref=xa.at[t, where, b], dst_ref=xa.at[t, where, b],
+            send_sem=(sent_right if right else sent_left).at[t],
+            recv_sem=ag_first.at[c, b] if t == 0 else ag_recv.at[c, b],
             device_id={"tensor": p + 1 if right else p - 1}, device_id_type=MESH)
 
     def sum_copy(t, c, d, right):
         return pltpu.make_async_remote_copy(
             src_ref=part.at[t, c, d], dst_ref=(from_left if right else from_right).at[t, c, d],
             send_sem=(sent_right if right else sent_left).at[t],
-            recv_sem=rl_recv.at[c, d - 1] if right else rr_recv.at[c, d],
+            recv_sem=rl_recv.at[t, c, d - 1] if right else rr_recv.at[t, c, d],
             device_id={"tensor": p + 1 if right else p - 1}, device_id_type=MESH)
 
-    def hop_copy(t, c):
+    def hop_copy(c):
         return pltpu.make_async_remote_copy(
-            src_ref=res.at[t, c], dst_ref=hop.at[t, c],
-            send_sem=hop_sent.at[t], recv_sem=hop_recv.at[t, c],
+            src_ref=res.at[1, c], dst_ref=hop.at[1, c],
+            send_sem=hop_sent.at[1], recv_sem=hop_recv.at[c],
             device_id={"section": s + 1}, device_id_type=MESH)
+
+    def first_hop():
+        return pltpu.make_async_remote_copy(
+            src_ref=res.at[0], dst_ref=hop.at[0], send_sem=hop_sent.at[0], recv_sem=hop_first,
+            device_id={"section": s + 1}, device_id_type=MESH)
+
+    def next_copy(c, q, side):
+        return pltpu.make_async_remote_copy(
+            src_ref=chosen.at[c], dst_ref=xa.at[1, c, q],
+            send_sem=next_sent.at[side + 1], recv_sem=ag_recv.at[c, q],
+            device_id={"section": s + 1, "tensor": q + side}, device_id_type=MESH)
+
+    def back_copies():
+        return [pltpu.make_async_remote_copy(
+            src_ref=src, dst_ref=dst, send_sem=back_sent.at[i], recv_sem=back_recv.at[i],
+            device_id={"section": s - 1}, device_id_type=MESH)
+            for i, (src, dst) in enumerate(((flag, flag_next), (mine, other)))]
 
     @scoped("gather_own")
     def gather_own(t, c):
@@ -189,12 +215,12 @@
         ).astype(jnp.bfloat16)
 
     @scoped("gather_step")
-    def gather_step(t, c, j):
+    def gather_step(c, j):
         b_left, b_right = p - 1 - j, p + 1 + j
 
         @pl.when(b_left >= 0)
         def _():
-            copy = gather_copy(t, c, b_left, True)
+            copy = gather_copy(0, c, b_left, True)
             copy.wait_recv()
 
             @pl.when(p < last)
@@ -203,20 +229,18 @@
 
         @pl.when(b_right <= last)
         def _():
-            copy = gather_copy(t, c, b_right, False)
+            copy = gather_copy(0, c, b_right, False)
             copy.wait_recv()
 
             @pl.when(p > 0)
             def _():
                 copy.start()
 
-        @pl.when(b_left >= 0)
-        def _():
-            normed(t, c, b_left)
-
-        @pl.when(b_right <= last)
-        def _():
-            normed(t, c, b_right)
+        for there, b in ((b_left >= 0, b_left), (b_right <= last, b_right)):
+            @pl.when(there)
+            def _():
+                normed(0, 2 * c, b)
+                normed(0, 2 * c + 1, b)
 
     @scoped("project")
     def project(part_of, begin, width):
@@ -310,29 +334,57 @@
 
         @pl.when(s < S - 1)
         def _():
-            hop_copy(t, c).start()
+            if t == 0:
+                chosen[c] = jnp.where(flag_next[0:1, 0:1] > 0.5, result.astype(jnp.float32),
+                                      other[c].astype(jnp.float32)).astype(jnp.bfloat16)
+                for side in (1, -1, 0):
+                    if 0 <= q + side <= last:
+                        next_copy(c, q, side).start()
+            else:
+                hop_copy(c).start()
         out[t, c] = result
 
     @scoped("arrived")
-    def arrived(t, c):
-        pltpu.make_async_copy(fresh_hbm.at[t, c], hop.at[t, c], hop_recv.at[t, c]).wait()
+    def arrived(c):
+        pltpu.make_async_copy(fresh_hbm.at[1, c], hop.at[1, c], hop_recv.at[c]).wait()
+
+    def sent_all(src, sem):
+        pltpu.make_async_remote_copy(
+            src_ref=src, dst_ref=src, send_sem=sem, recv_sem=hop_first,
+            device_id={"section": s + 1}, device_id_type=MESH).wait_send()
 
     def drain(t):
-        for right, there in ((True, p < last), (False, p > 0)):
+        for there, sem in ((p < last, sent_right), (p > 0, sent_left)):
             @pl.when(there)
             def _():
-                pltpu.make_async_remote_copy(
-                    src_ref=xa.at[t], dst_ref=xa.at[t],
-                    send_sem=(sent_right if right else sent_left).at[t], recv_sem=ag_recv.at[t, 0, 0],
-                    device_id={"tensor": p + 1 if right else p - 1}, device_id_type=MESH,
-                ).wait_send()
+                if t == 0:
+                    sent_all(xa.at[0], sem.at[0])
+                else:
+                    sent_all(xa.at[1, :, pl.ds(0, last)], sem.at[1])
+
+                    @pl.when(s == 0)
+                    def _():
+                        sent_all(res.at[1], sem.at[1])
 
         @pl.when(s < S - 1)
         def _():
-            pltpu.make_async_remote_copy(
-                src_ref=res.at[t], dst_ref=hop.at[t],
-                send_sem=hop_sent.at[t], recv_sem=hop_recv.at[t, 0],
-                device_id={"section": s + 1}, device_id_type=MESH).wait_send()
+            sent_all(res.at[t], hop_sent.at[t])
+            if t == 0:
+                sent_all(chosen, next_sent.at[1])
+
+                @pl.when(p > 0)
+                def _():
+                    sent_all(chosen, next_sent.at[0])
+
+                @pl.when(p < last)
+                def _():
+                    sent_all(chosen, next_sent.at[2])
+
+        if t == 0:
+            @pl.when(s > 0)
+            def _():
+                for copy in back_copies():
+                    copy.wait_send()
 
     def step(t, q, kind, c, d):
         if kind in ("up", "down"):
@@ -343,15 +395,20 @@
         elif kind == "project":
             project_part(c)
         elif kind == "next" and t == 0:
-            arrived(0, c)
-            xa[1, c, q] = jnp.where(first == second, hop[0, c], acts[second, c])
-            if q < last:
-                gather_copy(1, c, q, True).start()
-            if q > 0:
-                gather_copy(1, c, q, False).start()
+            @pl.when(s == 0)
+            def _():
+                xa[1, c, q] = jnp.where(first == second, hop[0, c], acts[second, c])
+                if q < last:
+                    gather_copy(1, c, q, True).start()
+                if q > 0:
+                    gather_copy(1, c, q, False).start()
+
+            @pl.when(s > 0)
+            def _():
+                gather_copy(1, c, q, q < last).wait_recv()
             normed(1, c, q)
         elif kind == "next":
-            arrived(1, c)
+            arrived(c)
             for j in range(2):
                 held[j, c] = jnp.where(
                     second == j, hop[1, c], jnp.where(first == j, hop[0, c], acts[j, c]))
@@ -371,30 +428,59 @@
         xa[0, c, p] = acts[first, c]
     with jax.named_scope("entry"):
         pl.semaphore_wait(barrier, sum(there.astype(jnp.int32) for there, _ in links))
-    for c in range(C):
+    for c in range(C // 2):
         gather_own(0, c)
 
+    @pl.when(s > 0)
+    def _():
+        for c in range(C):
+            mine[c] = acts[second, c]
+        flag[...] = jnp.full(flag.shape, jnp.where(first == second, 1.0, 0.0), jnp.float32)
+        for copy in back_copies():
+            copy.start()
     gain_in.wait()
     bias_in.wait()
     for c in range(C):
         normed(0, c, p)
     for j in range(last - 1):
-        for c in range(C):
-            gather_step(0, c, j)
+        for c in range(C // 2):
+            gather_step(c, j)
     wq_in.wait()
-    for c in range(C):
-        gather_step(0, c, last - 1)
-        if c % PROJECT == PROJECT - 1:
-            project_part(c // PROJECT)
+    for c in range(C // 2):
+        gather_step(c, last - 1)
+        if (2 * c + 1) % PROJECT == PROJECT - 1:
+            project_part(2 * c // PROJECT)
     wo_in.wait()
 
     for t in range(TICKS):
         attend_all(t)
+        if t == 0:
+            @pl.when(s < S - 1)
+            def _():
+                for copy in back_copies():
+                    copy.wait_recv()
+
+            @pl.when(s == 0)
+            def _():
+                pltpu.make_async_copy(fresh_hbm.at[0], hop.at[0], hop_first).wait()
         for q in range(T):
             @pl.when(p == q)
             def _():
+                owns, nexts = 0, 0
                 for event in orders[t][q]:
+                    if t == 1 and event[0] == "next":
+                        if nexts == 0:
+                            @pl.when(s > 0)
+                            def _():
+                                first_hop().wait_recv()
+                        nexts += 1
                     step(t, q, *event)
+                    if t == 0 and event[0] == "own":
+                        owns += 1
+                        if owns == C:
+                            @pl.when(s < S - 1)
+                            def _():
+                                first_hop().start()
         with jax.named_scope("drain"):
             drain(t)
 
@@ -440,9 +526,14 @@
             pltpu.VMEM(wide, jnp.bfloat16),
             pltpu.VMEM(block, jnp.bfloat16),
             pltpu.VMEM(block, jnp.bfloat16),
+            pltpu.VMEM(block[1:], jnp.bfloat16),
+            pltpu.VMEM(block[1:], jnp.bfloat16),
+            pltpu.VMEM((8, 128), jnp.float32),
+            pltpu.VMEM((8, 128), jnp.float32),
+            pltpu.VMEM(block[1:], jnp.bfloat16),
             *[pltpu.SemaphoreType.DMA] * 6,
-            sem(TICKS, CHUNKS, T), sem(CHUNKS, T - 1), sem(CHUNKS, T - 1),
-            sem(TICKS), sem(TICKS), sem(TICKS, CHUNKS), sem(TICKS),
+            sem(CHUNKS // 2, T), sem(CHUNKS, T), sem(TICKS, CHUNKS, T - 1), sem(TICKS, CHUNKS, T - 1),
+            sem(TICKS), sem(TICKS), pltpu.SemaphoreType.DMA, sem(CHUNKS), sem(TICKS), sem(3), sem(2), sem(2),
         ],
         compiler_params=pltpu.CompilerParams(
             collective_id=0, has_side_effects=True, vmem_limit_bytes=32 << 20),

time: 89.6 us -> 104 us (1.16); the launches traced: 88.4 us -> 104 us
  Pallas kernels: 87.6 us -> 103 us
    pallas_call x1, Pallas kernels: 86.6 us -> 102 us  [body(): pl.pallas_call(functools.partial(kernel, S, T), name='relay', out_shape=(...]
where the time goes in v4:
time: 104 us
  Pallas kernels  103 us (99%)
    pallas_call x1, Pallas kernels, body(): pl.pallas_call(functools.partial(kernel, S, T), name='relay', out_shape=(...  102 us

profile of v4, /device:TPU:1, one launch (start us, length us, event | category | flops | bytes accessed | tf_op | source)
XLA Modules:
  0.0 104.3 jit_solution(17575142366568475944)
XLA Ops:
  0.6 102.5 %relay.1 = (bf16[2,8,8,2048]{3,2,1,0:T(8,128)(2,1)S(1)}, bf16[2,8,8,2048]{3,2,1,0:T(8,128)(2,1)S(1)}) custom-call(s32[1,2]{1,0:T(1,128)} %order_hbm.1, bf16[2,8,8,2048]{3,2,1,0:T(8,128)(2,1)} %bitcast.10, bf16[2,8,8,2048]{3,2,1,0:T(8,128)(2,1)} %bitcast.11, f32[1,2048]{1,0:T(1,128)} %gain_hbm.1, f32[1,2048]{1,0:T(1,128)} %bias_hbm.1, ...), custom_call_target="tpu_custom_call" | custom-call | tf_op jit(solution)/shard_map/relay/pallas_call | solution.py:507
  103.1 1.0 store.1

commit v5 on v3

--- a/solution.py
+++ b/solution.py
@@ -19,7 +19,7 @@
 def plan(T, C, steps, queue):
     last, per = T - 1, C // steps
     wire, reach, hop_wire, hop_reach = 5.64 / C, 2.2, 2.82 / C, 2.6
-    add, norm, attend, project = 0.5 / C, 0.8 / C, 1.0, 1.7
+    add, norm, attend, project = 0.8 / C, 1.6 / C, 1.0, 2.0
     clock, free, arrivals = [0.0] * T, {}, {}
 
     def send(link, key, at, wire=wire, reach=reach):
@@ -59,7 +59,8 @@
             if kind in ("left", "right"):
                 need.append(("gather", p, c, d))
             if kind == "project" and any(
-                    e[0] in ("next", "left", "right") and e[1] // PROJECT == c for e in todo[p]):
+                    e[0] in ("next", "left", "right") and (e[1] // PROJECT == c or 0 < p < last)
+                    for e in todo[p]):
                 return None
             times = [arrivals.get(key) for key in need]
             return None if None in times else max([clock[p]] + times)
@@ -84,7 +85,7 @@
                     send((p, True), ("gather", p + 1, c, d), at)
                 if kind in ("next", "right") and p > 0:
                     send((p, False), ("gather", p - 1, c, d), at)
-                at += norm
+                at += norm if p in (0, last) else 0.02
             clock[p] = at
         orders.append(order)
     return orders
@@ -188,6 +189,16 @@
             centred * lax.rsqrt(spread + 1e-06) * gain[...] + bias[...]
         ).astype(jnp.bfloat16)
 
+    @scoped("normed")
+    def normed_chunks(t, begin):
+        @pl.loop(begin, begin + PROJECT)
+        def _(c):
+            values = xa[t, c].astype(jnp.float32).reshape(group, D)
+            centred = values - jnp.mean(values, axis=-1, keepdims=True)
+            spread = jnp.mean(centred * centred, axis=-1, keepdims=True)
+            scaled = centred * lax.rsqrt(spread + 1e-06) * gain[...] + bias[...]
+            norm[c] = scaled.reshape(T, rows, D).astype(jnp.bfloat16)
+
     @scoped("gather_step")
     def gather_step(t, c, j):
         b_left, b_right = p - 1 - j, p + 1 + j
@@ -218,23 +229,35 @@
         def _():
             normed(t, c, b_right)
 
+    def project(part_of, columns):
+        span = PROJECT * group
+        weights = [wq[:, cols] for cols in columns]
+        result = jnp.dot(
+            norm[PROJECT * part_of:PROJECT * (part_of + 1)].reshape(span, D),
+            weights[0] if len(weights) == 1 else jnp.concatenate(weights, axis=1),
+            preferred_element_type=jnp.float32,
+        ).astype(jnp.bfloat16)
+        at = 0
+        for cols in columns:
+            qkv[part_of * span:(part_of + 1) * span, cols] = result[:, at:at + cols.size]
+            at += cols.size
+
+    def head_columns(h, begin, width):
+        return pl.ds(pl.multiple_of(h * (3 * HD), HD) + begin, width)
+
     @scoped("project")
-    def project(part_of, begin, width):
-        span = PROJECT * group
-
+    def project_keys(part_of):
         @pl.loop(0, local_heads)
         def _(h):
-            cols = pl.ds(pl.multiple_of(h * (3 * HD), HD) + begin, width)
-            qkv[part_of * span:(part_of + 1) * span, cols] = jnp.dot(
-                norm[PROJECT * part_of:PROJECT * (part_of + 1)].reshape(span, D), wq[:, cols],
-                preferred_element_type=jnp.float32,
-            ).astype(jnp.bfloat16)
-
-    def project_keys(part_of):
-        project(part_of, HD, 2 * HD)
-
+            project(part_of, [head_columns(h, HD, 2 * HD)])
+
+    @scoped("project")
     def project_queries(part_of):
-        project(part_of, 0, HD)
+        pair = math.gcd(2, local_heads)
+
+        @pl.loop(0, local_heads // pair)
+        def _(h):
+            project(part_of, [head_columns(pair * h + i, 0, HD) for i in range(pair)])
 
     def project_part(part_of):
         project_keys(part_of)
@@ -341,6 +364,8 @@
         elif kind == "own":
             sum_own(t, c, q)
         elif kind == "project":
+            if 0 < q < last:
+                normed_chunks(1, c * PROJECT)
             project_part(c)
         elif kind == "next" and t == 0:
             arrived(0, c)
@@ -349,7 +374,8 @@
                 gather_copy(1, c, q, True).start()
             if q > 0:
                 gather_copy(1, c, q, False).start()
-            normed(1, c, q)
+            if q in (0, last):
+                normed(1, c, q)
         elif kind == "next":
             arrived(1, c)
             for j in range(2):
@@ -361,7 +387,8 @@
                 copy.wait_recv()
                 if (q < last) if kind == "left" else (q > 0):
                     copy.start()
-            normed(1, c, d)
+            if q in (0, last):
+                normed(1, c, d)
 
     with jax.named_scope("acts_wait"):
         order_in.wait()

time: 89.6 us -> 88.9 us (level)
  Pallas kernels: 87.6 us -> 86.6 us
    pallas_call x1, Pallas kernels: 86.6 us -> 85.6 us  [body(): pl.pallas_call(functools.partial(kernel, S, T), name='relay', out_shape=(...]
where the time goes in v5:
time: 88.9 us; the launch traced here: 87.4 us
  Pallas kernels  86.6 us (97%)
    pallas_call x1, Pallas kernels, body(): pl.pallas_call(functools.partial(kernel, S, T), name='relay', out_shape=(...  85.6 us

profile of v5, /device:TPU:1, one launch (start us, length us, event | category | flops | bytes accessed | tf_op | source)
XLA Modules:
  0.0 87.4 jit_solution(10977186733163694771)
XLA Ops:
  0.6 85.6 %relay.1 = (bf16[2,8,8,2048]{3,2,1,0:T(8,128)(2,1)S(1)}, bf16[2,8,8,2048]{3,2,1,0:T(8,128)(2,1)S(1)}) custom-call(s32[1,2]{1,0:T(1,128)} %order_hbm.1, bf16[2,8,8,2048]{3,2,1,0:T(8,128)(2,1)} %bitcast.10, bf16[2,8,8,2048]{3,2,1,0:T(8,128)(2,1)} %bitcast.11, f32[1,2048]{1,0:T(1,128)} %gain_hbm.1, f32[1,2048]{1,0:T(1,128)} %bias_hbm.1, ...), custom_call_target="tpu_custom_call" | custom-call | tf_op jit(solution)/shard_map/relay/pallas_call | solution.py:448
  86.2 1.0 %store.1 = (bf16[2,8,8,2048]{3,2,1,0:T(8,128)(2,1)}, bf16[2,8,8,2048]{3,2,1,0:T(8,128)(2,1)}) custom-call(bf16[2,8,8,2048]{3,2,1,0:T(8,128)(2,1)S(1)} %get-tuple-element.6.out, bf16[2,8,8,2048]{3,2,1,0:T(8,128)(2,1)S(1)} %get-tuple-element.7.held), custom_call_target="tpu_custom_call" | custom-call | tf_op jit(solution)/shard_map/store/pallas_call | solution.py:480

commit v6 on v5

--- a/solution.py
+++ b/solution.py
@@ -201,33 +201,24 @@
 
     @scoped("gather_step")
     def gather_step(t, c, j):
+        def forward(b, there, right):
+            @pl.when(there)
+            def _():
+                copy = gather_copy(t, c, b, right)
+                copy.wait_recv()
+
+                @pl.when((p < last) if right else (p > 0))
+                def _():
+                    copy.start()
+
+                @pl.when((p == 0) | (p == last))
+                def _():
+                    normed(t, c, b)
+
         b_left, b_right = p - 1 - j, p + 1 + j
-
-        @pl.when(b_left >= 0)
-        def _():
-            copy = gather_copy(t, c, b_left, True)
-            copy.wait_recv()
-
-            @pl.when(p < last)
-            def _():
-                copy.start()
-
-        @pl.when(b_right <= last)
-        def _():
-            copy = gather_copy(t, c, b_right, False)
-            copy.wait_recv()
-
-            @pl.when(p > 0)
-            def _():
-                copy.start()
-
-        @pl.when(b_left >= 0)
-        def _():
-            normed(t, c, b_left)
-
-        @pl.when(b_right <= last)
-        def _():
-            normed(t, c, b_right)
+        forward(b_right, (b_right <= last) & (p < T // 2), False)
+        forward(b_left, b_left >= 0, True)
+        forward(b_right, (b_right <= last) & (p >= T // 2), False)
 
     def project(part_of, columns):
         span = PROJECT * group
@@ -403,8 +394,12 @@
 
     gain_in.wait()
     bias_in.wait()
-    for c in range(C):
-        normed(0, c, p)
+    edge = (p == 0) | (p == last)
+
+    @pl.when(edge)
+    def _():
+        for c in range(C):
+            normed(0, c, p)
     for j in range(last - 1):
         for c in range(C):
             gather_step(0, c, j)
@@ -412,6 +407,9 @@
     for c in range(C):
         gather_step(0, c, last - 1)
         if c % PROJECT == PROJECT - 1:
+            @pl.when(~edge)
+            def _():
+                normed_chunks(0, c + 1 - PROJECT)
             project_part(c // PROJECT)
     wo_in.wait()
 

time: 88.9 us -> 88.5 us (level)
  no operation moved by 1% of the time
where the time goes in v6:
time: 88.5 us; the launch traced here: 87 us
  Pallas kernels  86.2 us (97%)
    pallas_call x1, Pallas kernels, body(): pl.pallas_call(functools.partial(kernel, S, T), name='relay', out_shape=(...  85.2 us

profile of v6, /device:TPU:1, one launch (start us, length us, event | category | flops | bytes accessed | tf_op | source)
XLA Modules:
  0.0 87.0 jit_solution(5978679738921956794)
XLA Ops:
  0.6 85.2 %relay.1 = (bf16[2,8,8,2048]{3,2,1,0:T(8,128)(2,1)S(1)}, bf16[2,8,8,2048]{3,2,1,0:T(8,128)(2,1)S(1)}) custom-call(s32[1,2]{1,0:T(1,128)} %order_hbm.1, bf16[2,8,8,2048]{3,2,1,0:T(8,128)(2,1)} %bitcast.10, bf16[2,8,8,2048]{3,2,1,0:T(8,128)(2,1)} %bitcast.11, f32[1,2048]{1,0:T(1,128)} %gain_hbm.1, f32[1,2048]{1,0:T(1,128)} %bias_hbm.1, ...), custom_call_target="tpu_custom_call" | custom-call | tf_op jit(solution)/shard_map/relay/pallas_call | solution.py:446
  85.9 1.0 %store.1 = (bf16[2,8,8,2048]{3,2,1,0:T(8,128)(2,1)}, bf16[2,8,8,2048]{3,2,1,0:T(8,128)(2,1)}) custom-call(bf16[2,8,8,2048]{3,2,1,0:T(8,128)(2,1)S(1)} %get-tuple-element.6.out, bf16[2,8,8,2048]{3,2,1,0:T(8,128)(2,1)S(1)} %get-tuple-element.7.held), custom_call_target="tpu_custom_call" | custom-call | tf_op jit(solution)/shard_map/store/pallas_call | solution.py:478

commit v7 on v6

--- a/solution.py
+++ b/solution.py
@@ -111,7 +111,7 @@
 def kernel(
     S, T, order_hbm, acts_hbm, fresh_hbm, gain_hbm, bias_hbm, wq_hbm, wo_hbm, out, held,
     order, acts, gain, bias, wq, wo, xa, norm, qkv, attn, part, from_left, from_right, res, hop,
-    order_sem, acts_sem, gain_sem, bias_sem, wq_sem, wo_sem, ag_recv, rl_recv, rr_recv,
+    order_sem, acts_sem, gain_sem, bias_sem, wq_sem, wo_sem, ag_first, ag_recv, rl_recv, rr_recv,
     sent_right, sent_left, hop_recv, hop_sent,
 ):
     C = CHUNKS
@@ -152,9 +152,11 @@
         return lambda f: jax.named_scope(name)(f)
 
     def gather_copy(t, c, b, right):
+        where = pl.ds(2 * c, 2) if t == 0 else c
         return pltpu.make_async_remote_copy(
-            src_ref=xa.at[t, c, b], dst_ref=xa.at[t, c, b],
-            send_sem=(sent_right if right else sent_left).at[t], recv_sem=ag_recv.at[t, c, b],
+            src_ref=xa.at[t, where, b], dst_ref=xa.at[t, where, b],
+            send_sem=(sent_right if right else sent_left).at[t],
+            recv_sem=ag_first.at[c, b] if t == 0 else ag_recv.at[c, b],
             device_id={"tensor": p + 1 if right else p - 1}, device_id_type=MESH)
 
     def sum_copy(t, c, d, right):
@@ -213,7 +215,8 @@
 
                 @pl.when((p == 0) | (p == last))
                 def _():
-                    normed(t, c, b)
+                    normed(t, 2 * c, b)
+                    normed(t, 2 * c + 1, b)
 
         b_left, b_right = p - 1 - j, p + 1 + j
         forward(b_right, (b_right <= last) & (p < T // 2), False)
@@ -337,7 +340,7 @@
             def _():
                 pltpu.make_async_remote_copy(
                     src_ref=xa.at[t], dst_ref=xa.at[t],
-                    send_sem=(sent_right if right else sent_left).at[t], recv_sem=ag_recv.at[t, 0, 0],
+                    send_sem=(sent_right if right else sent_left).at[t], recv_sem=ag_recv.at[0, 0],
                     device_id={"tensor": p + 1 if right else p - 1}, device_id_type=MESH,
                 ).wait_send()
 
@@ -389,7 +392,7 @@
         xa[0, c, p] = acts[first, c]
     with jax.named_scope("entry"):
         pl.semaphore_wait(barrier, sum(there.astype(jnp.int32) for there, _ in links))
-    for c in range(C):
+    for c in range(C // 2):
         gather_own(0, c)
 
     gain_in.wait()
@@ -401,11 +404,11 @@
         for c in range(C):
             normed(0, c, p)
     for j in range(last - 1):
-        for c in range(C):
+        for c in range(C // 2):
             gather_step(0, c, j)
     wq_in.wait()
-    for c in range(C):
-        gather_step(0, c, last - 1)
+    for c in range(1, C, 2):
+        gather_step(0, c // 2, last - 1)
         if c % PROJECT == PROJECT - 1:
             @pl.when(~edge)
             def _():
@@ -466,7 +469,7 @@
             pltpu.VMEM(block, jnp.bfloat16),
             pltpu.VMEM(block, jnp.bfloat16),
             *[pltpu.SemaphoreType.DMA] * 6,
-            sem(TICKS, CHUNKS, T), sem(CHUNKS, T - 1), sem(CHUNKS, T - 1),
+            sem(CHUNKS // 2, T), sem(CHUNKS, T), sem(CHUNKS, T - 1), sem(CHUNKS, T - 1),
             sem(TICKS), sem(TICKS), sem(TICKS, CHUNKS), sem(TICKS),
         ],
         compiler_params=pltpu.CompilerParams(

time: 88.5 us -> 87.7 us (level)
  Pallas kernels: 86.2 us -> 85.3 us
    pallas_call x1, Pallas kernels: 85.2 us -> 84.3 us  [body(): pl.pallas_call(functools.partial(kernel, S, T), name='relay', out_shape=(...]
where the time goes in v7:
time: 87.7 us; the launch traced here: 86.1 us
  Pallas kernels  85.3 us (97%)
    pallas_call x1, Pallas kernels, body(): pl.pallas_call(functools.partial(kernel, S, T), name='relay', out_shape=(...  84.3 us

profile of v7, /device:TPU:1, one launch (start us, length us, event | category | flops | bytes accessed | tf_op | source)
XLA Modules:
  0.0 86.1 jit_solution(4017403910889426417)
XLA Ops:
  0.6 84.3 %relay.1 = (bf16[2,8,8,2048]{3,2,1,0:T(8,128)(2,1)S(1)}, bf16[2,8,8,2048]{3,2,1,0:T(8,128)(2,1)S(1)}) custom-call(s32[1,2]{1,0:T(1,128)} %order_hbm.1, bf16[2,8,8,2048]{3,2,1,0:T(8,128)(2,1)} %bitcast.10, bf16[2,8,8,2048]{3,2,1,0:T(8,128)(2,1)} %bitcast.11, f32[1,2048]{1,0:T(1,128)} %gain_hbm.1, f32[1,2048]{1,0:T(1,128)} %bias_hbm.1, ...), custom_call_target="tpu_custom_call" | custom-call | tf_op jit(solution)/shard_map/relay/pallas_call | solution.py:449
  85.0 1.0 %store.1 = (bf16[2,8,8,2048]{3,2,1,0:T(8,128)(2,1)}, bf16[2,8,8,2048]{3,2,1,0:T(8,128)(2,1)}) custom-call(bf16[2,8,8,2048]{3,2,1,0:T(8,128)(2,1)S(1)} %get-tuple-element.6.out, bf16[2,8,8,2048]{3,2,1,0:T(8,128)(2,1)S(1)} %get-tuple-element.7.held), custom_call_target="tpu_custom_call" | custom-call | tf_op jit(solution)/shard_map/store/pallas_call | solution.py:481
